TPU v7x, 8 devices: a whole 2x2x1 slice. The times are simulated.
8 devices in a mesh: dp: 1 (over z), tp: 2 (over y), sp: 4 (over x, core).
Axes of the slice: x: 2, y: 2, z: 1, core: 2. Of those that a mesh axis runs over, the one named last changes fastest.
Arguments:
- hidden: bfloat16 [64, 4096], P('dp')
- norm_gain: float32 [4096], replicated
- w_query: bfloat16 [4096, 4096], P(None, 'tp')
- w_key: bfloat16 [4096, 1024], P(None, 'tp')
- w_value: bfloat16 [4096, 1024], P(None, 'tp')
- w_out: bfloat16 [4096, 4096], P('tp')
- k_cache: bfloat16 [64, 1024, 8, 128], P('dp', 'sp', 'tp')
- v_cache: bfloat16 [64, 1024, 8, 128], P('dp', 'sp', 'tp')
- positions: int32 [64], P('dp')
Outputs:
- output 1: bfloat16 [64, 4096], P('dp')
- output 2: bfloat16 [64, 1024, 8, 128], P('dp', 'sp', 'tp')
- output 3: bfloat16 [64, 1024, 8, 128], P('dp', 'sp', 'tp')
All inputs are finite; a program needn't handle non-finite values.
Results may differ from a plain program's by a relative error of at most 0.00414588.
Values sent between devices are 32-bit elements.
A program may use at most 1 GiB of HBM per device.

v0:
```python
import jax
import jax.numpy as jnp
from jax import lax
from jax.sharding import PartitionSpec as P

ROPE_BASE = 1000000.0
EPS = 1e-5
NEG_BIG = -1e30


def rotary(tensor, positions):
    half_dim = tensor.shape[-1] // 2
    inv_freq = 1.0 / (ROPE_BASE ** (jnp.arange(half_dim, dtype=jnp.float32) * 2.0 / tensor.shape[-1]))
    angles = positions.astype(jnp.float32)[:, None, None] * inv_freq[None, None, :]
    cosine = jnp.cos(angles)
    sine_val = jnp.sin(angles)
    first_half = tensor[..., :half_dim]
    second_half = tensor[..., half_dim:]
    return jnp.concatenate([first_half * cosine - second_half * sine_val, first_half * sine_val + second_half * cosine], axis=-1)


def solution(mesh):
    def local_step(hidden, norm_gain, w_query, w_key, w_value, w_out, k_cache, v_cache, positions):
        batch_size, seq_local, kv_local, head_dim = k_cache.shape
        q_local = w_query.shape[1] // head_dim
        group_size = q_local // kv_local
        resid_f32 = hidden.astype(jnp.float32)
        normed = (resid_f32 * lax.rsqrt(jnp.mean(resid_f32 * resid_f32, axis=-1, keepdims=True) + EPS) * norm_gain).astype(jnp.bfloat16)
        q_proj = jnp.dot(normed, w_query, preferred_element_type=jnp.float32).reshape(batch_size, q_local, head_dim)
        k_proj = jnp.dot(normed, w_key, preferred_element_type=jnp.float32).reshape(batch_size, kv_local, head_dim)
        v_new = jnp.dot(normed, w_value, preferred_element_type=jnp.float32).astype(jnp.bfloat16).reshape(batch_size, kv_local, head_dim)
        q_rot = rotary(q_proj, positions).astype(jnp.bfloat16).reshape(batch_size, kv_local, group_size, head_dim)
        k_new = rotary(k_proj, positions).astype(jnp.bfloat16)
        slot_pos = lax.axis_index("sp") * seq_local + jnp.arange(seq_local)
        slot_mask = (slot_pos[None, :] == positions[:, None])[:, :, None, None]
        k_updated = jnp.where(slot_mask, k_new[:, None], k_cache)
        v_updated = jnp.where(slot_mask, v_new[:, None], v_cache)
        scores = jnp.einsum("bkgd,bskd->bkgs", q_rot, k_updated, preferred_element_type=jnp.float32) * (head_dim ** -0.5)
        valid_mask = (slot_pos[None, :] <= positions[:, None])[:, None, None, :]
        scores = jnp.where(valid_mask, scores, NEG_BIG)
        local_max = jnp.max(scores, axis=-1, keepdims=True)
        exp_weights = jnp.where(valid_mask, jnp.exp(scores - local_max), 0.0)
        local_sum = jnp.sum(exp_weights, axis=-1, keepdims=True)
        local_acc = jnp.einsum("bkgs,bskd->bkgd", exp_weights.astype(jnp.bfloat16), v_updated, preferred_element_type=jnp.float32)
        block_stats = jnp.concatenate([local_acc, local_sum, local_max], axis=-1)
        gathered = lax.all_gather(block_stats, "sp")
        all_max = gathered[..., head_dim + 1:]
        global_max = jnp.max(all_max, axis=0)
        rescale = jnp.exp(all_max - global_max)
        total_sum = jnp.sum(gathered[..., head_dim:head_dim + 1] * rescale, axis=0)
        total_acc = jnp.sum(gathered[..., :head_dim] * rescale, axis=0)
        attn_out = (total_acc / total_sum).astype(jnp.bfloat16).reshape(batch_size, q_local * head_dim)
        part_proj = jnp.dot(attn_out, w_out, preferred_element_type=jnp.float32)
        proj_out = lax.psum(part_proj, "tp")
        return (resid_f32 + proj_out).astype(jnp.bfloat16), k_updated, v_updated

    cache_spec = P("dp", "sp", "tp", None)
    specs_in = (P("dp", None), P(None), P(None, "tp"), P(None, "tp"), P(None, "tp"), P("tp", None), cache_spec, cache_spec, P("dp"))
    specs_out = (P("dp", None), cache_spec, cache_spec)
    return jax.shard_map(local_step, mesh=mesh, in_specs=specs_in, out_specs=specs_out, check_vma=False)
```

profile of v0, /device:TPU:0, one launch (start us, length us, event | category | flops | bytes accessed | tf_op | source)
XLA Modules:
  0.0 177.5 jit_solution(1161695125420943661)
XLA Ops:
  7.2 0.7 convert_element_type.35
  7.9 1.2 fusion.11
  9.2 0.7 broadcast_compare_fusion.1
  9.9 3.3 %convolution_convert_fusion = bf16[64,512]{1,0:T(8,128)(2,1)S(1)} fusion(bf16[4096,512]{1,0:T(8,128)(2,1)} %param.13, bf16[64,4096]{1,0:T(8,128)(2,1)} %param.9, f32[4096]{0:T(1024)} %param.10, f32[64]{0:T(128)S(1)} %add_rsqrt_fusion), kind=kOutput, calls=%fused_computation.13 | convolution fusion | flops 269516800 | bytes 4800768 | tf_op jit(solution)/shard_map/dot_general | solution.py:31
  13.2 3.3 %fusion.28 = f32[64,512]{1,0:T(8,128)S(1)} fusion(bf16[4096,512]{1,0:T(8,128)(2,1)} %param.12, bf16[64,4096]{1,0:T(8,128)(2,1)} %param.9, f32[4096]{0:T(1024)} %param.10, f32[64]{0:T(128)S(1)} %add_rsqrt_fusion), kind=kOutput, calls=%fused_computation.47 | convolution fusion | flops 269484032 | bytes 4866304 | tf_op jit(solution)/shard_map/dot_general | solution.py:30
  16.5 9.1 %convolution_bitcast_fusion = f32[8,8,16,128]{3,1,2,0:T(8,128)S(1)} fusion(bf16[4096,2048]{1,0:T(8,128)(2,1)} %param.11, bf16[64,4096]{1,0:T(8,128)(2,1)} %param.9, f32[4096]{0:T(1024)} %param.10, f32[64]{0:T(128)S(1)} %add_rsqrt_fusion), kind=kOutput, calls=%fused_computation.12 | convolution fusion | flops 1074790400 | bytes 17842432 | tf_op jit(solution)/shard_map/dot_general | solution.py:29
  25.6 0.1 copy.39
  25.7 0.2 multiply_cosine_fusion
  25.9 0.2 subtract_convert_fusion.1
  26.1 0.2 subtract_convert_fusion
  26.3 0.1 pad_maximum_fusion.1
  26.4 26.1 %broadcast_select_fusion = (bf16[64,256,4,128]{3,2,1,0:T(4,128)(2,1)}, bf16[64,256,4,128]{3,2,1,0:T(4,128)(2,1)}) fusion(bf16[64,256,4,128]{3,2,1,0:T(4,128)(2,1)} %param.16, pred[64,256]{1,0:T(8,128)(4,1)S(1)} %get-tuple-element.15, bf16[64,4,128]{2,1,0:T(4,128)(2,1)S(1)} %broadcast_in_dim.69, bf16[64,256,4,128]{3,2,1,0:T(4,128)(2,1)} %param.15, ...), kind=kLoop, calls=%fused_computation.4 | loop fusion | flops 16777216 | bytes 67256320 | tf_op jit(solution)/shard_map/jit(_where)/select_n | solution.py:37
  52.5 10.4 %fusion.32 = (f32[64,4,4]{2,1,0:T(4,128)S(1)}, f32[64,4,4,256]{3,2,1,0:T(4,128)S(1)}) fusion(bf16[64,256,4,128]{3,2,1,0:T(4,128)(2,1)} %get-tuple-element.13, bf16[64,4,4,64]{3,2,1,0:T(4,128)(2,1)S(1)} %bitcast.21, bf16[64,4,4,64]{3,2,1,0:T(4,128)(2,1)S(1)} %bitcast.20, pred[64,256]{1,0:T(8,128)(4,1)S(1)} %get-tuple-element.14), kind=kOutput, calls=%fused_computation.50 | convolution fusion | flops 68418560 | bytes 18108416 | tf_op jit(solution)/shard_map/bkgd,bskd->bkgs/dot_general | solution.py:38
  62.9 0.8 fusion.15
  63.7 8.1 %fusion = f32[64,4,4,128]{3,2,1,0:T(4,128)S(1)} fusion(bf16[64,256,4,128]{3,2,1,0:T(4,128)(2,1)} %get-tuple-element.12, f32[64,4,4,256]{3,2,1,0:T(4,128)S(1)} %get-tuple-element.19, f32[64,4,4]{2,1,0:T(4,128)S(1)} %get-tuple-element.18, pred[64,256]{1,0:T(8,128)(4,1)S(1)} %get-tuple-element.14), kind=kOutput, calls=%fused_computation | convolution fusion | flops 67895296 | bytes 18370560 | tf_op jit(solution)/shard_map/bkgs,bskd->bkgd/dot_general | solution.py:44
  71.8 1.7 copy.26
  73.5 1.7 copy.27
  75.2 1.4 pad_maximum_fusion
  76.6 0.0 all-reduce.2.cloned.1.call-start
  76.6 34.4 %all-gather.3.cloned.1.call-done = f32[256,4,4,130]{3,2,1,0:T(4,128)} async-done(((f32[64,4,4,130]{3,2,1,0:T(4,128)}), f32[256,4,4,130]{3,2,1,0:T(4,128)}) %all-gather.3.cloned.1.call-update) | async-done | bytes 2129936 | tf_op jit(solution)/shard_map/all_gather | solution.py:46
  111.1 5.4 %fusion.31 = (f32[4,64,4,4,1]{4,3,2,1,0:T(4,128)}, f32[64,4,4]{2,1,0:T(4,128)S(1)}, f32[4,64,4,4,1]{4,3,2,1,0:T(4,128)S(1)}) fusion(f32[4,64,4,4,130]{4,3,2,1,0:T(4,128)} %bitcast.15), kind=kLoop, calls=%fused_computation.49 | loop fusion | flops 3072 | bytes 69632 | tf_op jit(solution)/shard_map/slice | solution.py:50
  116.5 2.3 %copy.37 = f32[4,64,4,4,1]{1,3,4,2,0:T(4,128)S(1)} copy(f32[4,64,4,4,1]{4,3,2,1,0:T(4,128)} %get-tuple-element.3) | data formatting | bytes 32768
  118.8 0.1 copy.38
  118.9 1.1 copy.36
  120.0 0.1 copy.31
  120.2 0.3 copy.29
  120.4 3.3 %fusion.4 = f32[64,4,4,128]{3,2,1,0:T(4,128)S(1)} fusion(f32[4,64,4,4,130]{4,3,2,1,0:T(4,128)} %bitcast.16, f32[4,64,4,4]{3,2,1,0:T(4,128)S(1)} %copy.29), kind=kLoop, calls=%fused_computation.7 | loop fusion | flops 917504 | bytes 2637824 | tf_op jit(solution)/shard_map/reduce_sum | solution.py:51
  123.7 0.3 divide_convert_fusion
  124.1 0.2 convert_element_type.39
  124.3 9.8 %fusion.33 = f32[64,4096]{1,0:T(8,128)} fusion(bf16[64,2048]{1,0:T(8,128)(2,1)S(1)} %convert_element_type.39, bf16[2048,4096]{1,0:T(8,128)(2,1)} %param.14), kind=kOutput, calls=%fused_computation.51 | convolution fusion | flops 1073741824 | bytes 18087936 | tf_op jit(solution)/shard_map/dot_general | solution.py:53
  134.1 34.4 %all-reduce.2.cloned.1.call-done = f32[64,4096]{1,0:T(8,128)} async-done(((f32[64,4096]{1,0:T(8,128)}), f32[64,4096]{1,0:T(8,128)}) %all-reduce.2.cloned.1.call-update) | async-done | bytes 1048592 | tf_op jit(solution)/shard_map/psum | solution.py:54
  168.5 2.1 %fusion.14 = bf16[64,4096]{1,0:T(8,128)(2,1)} fusion(f32[64,4096]{1,0:T(8,128)} %all-reduce.2.cloned.1.call-done, bf16[64,4096]{1,0:T(8,128)(2,1)S(1)} %copy-done), kind=kLoop, calls=%fused_computation.18 | loop fusion | flops 786432 | bytes 2097152 | tf_op jit(solution)/shard_map/convert_element_type | solution.py:55
  (11 shorter events, 0.2 us)
Async XLA Ops:
  7.2 103.9 %all-gather.3.cloned.1.call-start = ((), (), s32[]{:S(2)}) async-start(), calls=%async_computation.1 | async-start | bytes 5242880 | tf_op jit(solution)/shard_map/all_gather | solution.py:46
  76.6 91.9 %all-reduce.2.cloned.1.call-start = ((), (), s32[]{:S(2)}) async-start(), calls=%async_computation | async-start | bytes 2097152 | tf_op jit(solution)/shard_map/psum | solution.py:54
  118.8 49.7 %copy-start = (bf16[64,4096]{1,0:T(8,128)(2,1)S(1)}, bf16[64,4096]{1,0:T(8,128)(2,1)}, u32[]{:S(2)}) copy-start(bf16[64,4096]{1,0:T(8,128)(2,1)} %param.9) | copy-start | bytes 1572868
Sparse Core Ops, SparseCore 0:
  76.7 34.3 all-gather.2
  134.2 34.2 all-reduce.1
where the time goes:
time: 178 us; the launch traced here: 177 us
  waiting for transfers between devices  68.9 us (39%)
  matrix products  43.9 us (25%)
  other arithmetic  42.8 us (24%)
  between operations  14.2 us (8%)
  local copies, waits for them, and re-layouts  7.57 us (4%)
    all_gather x1, waiting for transfers between devices, local_step(): gathered = lax.all_gather(block_stats, 'sp')  34.4 us
    psum x1, waiting for transfers between devices, local_step(): proj_out = lax.psum(part_proj, 'tp')  34.4 us
    select_n x1, other arithmetic, local_step(): v_updated = jnp.where(slot_mask, v_new[:, None], v_cache)  26.1 us
    dot_general x1, matrix products, local_step(): jnp.einsum('bkgd,bskd->bkgs', q_rot, k_updated, preferred_element_type=jn...  10.4 us
    dot_general x1, matrix products, local_step(): part_proj = jnp.dot(attn_out, w_out, preferred_element_type=jnp.float32)  9.83 us
    dot_general x1, matrix products, local_step(): jnp.dot(normed, w_query, preferred_element_type=jnp.float32)  9.06 us
    dot_general x1, matrix products, local_step(): jnp.einsum('bkgs,bskd->bkgd', exp_weights.astype(jnp.bfloat16), v_updated...  8.11 us
    slice x1, other arithmetic, local_step(): total_sum = jnp.sum(gathered[..., head_dim:head_dim + 1] * rescale, axis=0)  5.41 us
  transfers between devices with their start and end apart: 2, of which 2 were waited for; matrix products, arithmetic and copies ran while one was open for 0% of the time, Pallas kernels for 0%

commit v1 on v0

v1 whole, which is shorter than its diff:
```python
import functools
import math

import jax
import jax.numpy as jnp
from jax import lax
from jax.experimental import pallas as pl
from jax.experimental.pallas import tpu as pltpu
from jax.sharding import PartitionSpec as P

ROPE_BASE = 1000000.0
EPS = 1e-5
NEG_BIG = -1e30

B = 64
D = 4096
HD = 128
QL = 16
KVL = 4
SL = 256
RB = SL * KVL
QW, KW = QL * HD, KVL * HD
NW = QW + 2 * KW
WROWS = 256
NWC = D // WROWS
NSLOT = 6
CB = 4
NCC = B // CB
AHEAD = 5
HB = B // 2
STAT = HB * 8 + 8
SCALE = HD ** -0.5 * math.log2(math.e)
F32, BF16 = jnp.float32, jnp.bfloat16
VM = pltpu.VMEM
ANY = pl.ANY


def attn_kernel(pos_ref, hid_ref, gain_ref, cos_ref, sin_ref, wq, wk, wv, kc, vc,
                kout, vout, keep_ref, send_ref,
                wbuf, acc_s, r_s, q_s, kn_s, vn_s, slot_s, ml_s, wsem, ksem, vsem):
    sp = lax.axis_index("sp")
    core = lax.rem(sp, 2)
    off = sp * SL

    def weight_copies(i, slot):
        rows = pl.ds(i * WROWS, WROWS)
        return (
            pltpu.make_async_copy(wq.at[rows], wbuf.at[slot, :, pl.ds(0, QW)], wsem.at[slot, 0]),
            pltpu.make_async_copy(wk.at[rows], wbuf.at[slot, :, pl.ds(QW, KW)], wsem.at[slot, 1]),
            pltpu.make_async_copy(wv.at[rows], wbuf.at[slot, :, pl.ds(QW + KW, KW)], wsem.at[slot, 2]),
        )

    def cache_copies(j):
        rows = pl.ds(j * (CB * RB), CB * RB)
        return (
            pltpu.make_async_copy(kc.at[rows], kout.at[rows], ksem.at[j]),
            pltpu.make_async_copy(vc.at[rows], vout.at[rows], vsem.at[j]),
        )

    def start(copies):
        for c in copies:
            c.start()

    def wait(copies):
        for c in copies:
            c.wait()

    for i in range(NSLOT):
        start(weight_copies(i, i))

    hid = hid_ref[...].astype(F32)
    inv = lax.rsqrt(jnp.mean(hid * hid, axis=-1, keepdims=True) + EPS)
    normed = (hid * inv * gain_ref[...]).astype(BF16)
    for i in range(NWC):
        r_s[i] = normed[:, i * WROWS:(i + 1) * WROWS]
    col = lax.broadcasted_iota(jnp.int32, (QL, RB), 1)
    row = lax.broadcasted_iota(jnp.int32, (QL, RB), 0)
    slot_s[...] = jnp.where(col % KVL == row // (QL // KVL), col // KVL, 1 << 20)
    acc_s[...] = jnp.zeros_like(acc_s)

    def weight_step(i, carry):
        slot = lax.rem(i, NSLOT)
        wait(weight_copies(i, slot))
        acc_s[...] += jnp.dot(r_s[i], wbuf[slot], preferred_element_type=F32)

        @pl.when(i + NSLOT < NWC)
        def _():
            start(weight_copies(i + NSLOT, slot))

        @pl.when(i + NSLOT >= NWC)
        def _():
            start(cache_copies(i + NSLOT - NWC))

        return carry

    lax.fori_loop(0, NWC, weight_step, 0)

    cosf, sinf = cos_ref[...], sin_ref[...]
    for h in range(QL):
        x = acc_s[:, h * HD:(h + 1) * HD]
        q_s[pl.ds(h, B, stride=QL), :] = x * cosf + pltpu.roll(x, HD // 2, 1) * sinf
    for h in range(KVL):
        x = acc_s[:, QW + h * HD:QW + (h + 1) * HD]
        kx = x * cosf + pltpu.roll(x, HD // 2, 1) * sinf
        vx = acc_s[:, QW + KW + h * HD:QW + KW + (h + 1) * HD]
        for t in range(4):
            kn_s[pl.ds(t * KVL + h, B, stride=16), :] = kx
            vn_s[pl.ds(t * KVL + h, B, stride=16), :] = vx

    ml_s[...] = jnp.zeros_like(ml_s)
    lane = lax.broadcasted_iota(jnp.int32, (QL, HD), 1)
    brow = lax.broadcasted_iota(jnp.int32, (16, HD), 0) // KVL

    def cache_step(j, carry):
        @pl.when(j + NSLOT < NCC)
        def _():
            start(cache_copies(j + NSLOT))

        wait(cache_copies(j))
        for t in range(CB):
            b = j * CB + t
            p = pos_ref[b] - off
            base = pl.multiple_of(b * RB, RB)
            pc = jnp.clip(p, 0, SL - 1)
            at = pl.multiple_of(base + (pc // 4) * 16, 16)
            hit = brow == jnp.where((p >= 0) & (p < SL), pc % 4, -1)
            b16 = pl.multiple_of(b * 16, 16)
            kout[pl.ds(at, 16), :] = jnp.where(hit, kn_s[pl.ds(b16, 16), :].astype(BF16), kout[pl.ds(at, 16), :])
            vout[pl.ds(at, 16), :] = jnp.where(hit, vn_s[pl.ds(b16, 16), :].astype(BF16), vout[pl.ds(at, 16), :])
        for t in range(CB):
            b = j * CB + t
            p = pos_ref[b] - off
            base = pl.multiple_of(b * RB, RB)
            b16 = pl.multiple_of(b * 16, 16)
            q = q_s[pl.ds(b16, QL), :].astype(BF16)
            s = lax.dot_general(q, kout[pl.ds(base, RB), :], (((1,), (1,)), ((), ())), preferred_element_type=F32)
            valid = slot_s[...] <= p
            s = jnp.where(valid, s * SCALE, NEG_BIG)
            m = jnp.max(s, axis=-1, keepdims=True)
            e = jnp.where(valid, jnp.exp2(s - m), 0.0)
            l = jnp.sum(e, axis=-1, keepdims=True)
            o = jnp.dot(e.astype(BF16), vout[pl.ds(base, RB), :], preferred_element_type=F32)
            bh, bl = b // HB, lax.rem(b, HB)
            at = pl.ds(pl.multiple_of(bl * 8, 8), 8)
            keep_ref[bh, at, :] = jnp.where(core == 0, o[0:8], o[8:16])
            send_ref[bh, at, :] = jnp.where(core == 0, o[8:16], o[0:8])
            ml = ml_s[...]
            ml = jnp.where(lane == b, m, ml)
            ml_s[...] = jnp.where(lane == b + B, l, ml)
        return carry

    lax.fori_loop(0, NCC, cache_step, 0)
    ml = ml_s[...]
    for bh in range(2):
        keep_ref[bh, pl.ds(HB * 8, 8), :] = jnp.where(core == 0, ml[0:8], ml[8:16])
        send_ref[bh, pl.ds(HB * 8, 8), :] = jnp.where(core == 0, ml[8:16], ml[0:8])


def weights_of(ml_a, ml_b):
    m = jnp.maximum(ml_a, ml_b)
    wa, wb = jnp.exp2(ml_a - m), jnp.exp2(ml_b - m)
    l = wa * pltpu.roll(ml_a, B, 1) + wb * pltpu.roll(ml_b, B, 1)
    return m, l, wa, wb


def merge_kernel(keep_in, recv_in, keep_ref, send_ref):
    chip = lax.axis_index("sp") // 2
    lane = lax.broadcasted_iota(jnp.int32, (8, HD), 1)
    ml = pl.ds(HB * 8, 8)
    m, l, wa, wb = weights_of(keep_in[0, ml, :], recv_in[0, ml, :])
    new = jnp.where(lane < B, m, pltpu.roll(l, B, 1))
    keep_ref[ml, :] = new
    send_ref[ml, :] = new
    for b in range(HB):
        at = pl.ds(b * 8, 8)
        r = []
        for h in range(2):
            c = h * HB + b
            r.append(wa[:, c:c + 1] * keep_in[h, at, :] + wb[:, c:c + 1] * recv_in[h, at, :])
        keep_ref[at, :] = jnp.where(chip == 0, r[0], r[1])
        send_ref[at, :] = jnp.where(chip == 0, r[1], r[0])


def finish_kernel(keep_in, recv_in, o_ref):
    chip = lax.axis_index("sp") // 2
    ml = pl.ds(HB * 8, 8)
    m, l, wa, wb = weights_of(keep_in[ml, :], recv_in[ml, :])
    lane = lax.broadcasted_iota(jnp.int32, (8, HD), 1)
    inv = 1.0 / jnp.where(lane < B, l, 1.0)
    wa, wb = wa * inv, wb * inv
    wa = jnp.where(chip == 0, wa, pltpu.roll(wa, HD - HB, 1))
    wb = jnp.where(chip == 0, wb, pltpu.roll(wb, HD - HB, 1))
    for b in range(HB):
        at = pl.ds(b * 8, 8)
        o = wa[:, b:b + 1] * keep_in[at, :] + wb[:, b:b + 1] * recv_in[at, :]
        o_ref[at, :] = o.astype(BF16).astype(F32)


OC = 8


def out_kernel(own_ref, sib_ref, wo, y0_ref, y1_ref, obuf, lhs, sem):
    core = lax.rem(lax.axis_index("sp"), 2)
    half = QW // 2
    cols = pl.ds(pl.multiple_of(core * (D // 2), D // 2), D // 2)

    def copy(i):
        r0 = jnp.where(i < OC // 2, core, 1 - core) * half + lax.rem(i, OC // 2) * (QW // OC)
        rows = pl.ds(pl.multiple_of(r0, QW // OC), QW // OC)
        return pltpu.make_async_copy(wo.at[rows, cols], obuf.at[i], sem.at[i])

    for i in range(OC):
        copy(i).start()
    for h in range(8):
        lhs[:, h * HD:(h + 1) * HD] = own_ref[pl.ds(h, HB, stride=8), :].astype(BF16)
        lhs[:, half + h * HD:half + (h + 1) * HD] = sib_ref[pl.ds(h, HB, stride=8), :].astype(BF16)
    acc = None
    n = QW // OC
    for i in range(OC):
        copy(i).wait()
        d = jnp.dot(lhs[:, i * n:(i + 1) * n], obuf[i], preferred_element_type=F32)
        acc = d if acc is None else acc + d
    y0_ref[...] = acc[:, :D // 4]
    y1_ref[...] = acc[:, D // 4:]


def write_kernel(src, dst, sem):
    n = src.shape[0] // 8
    copies = [pltpu.make_async_copy(src.at[pl.ds(i * n, n)], dst.at[pl.ds(i * n, n)], sem.at[i]) for i in range(8)]
    for c in copies:
        c.start()
    for c in copies:
        c.wait()


def final_kernel(hid_ref, own0, own1, xr0, xr1, sown0, sown1, sxr0, sxr1, out_ref):
    sp = lax.axis_index("sp")
    chip, core = sp // 2, lax.rem(sp, 2)
    half, quart = D // 2, D // 4
    for mine, parts in ((True, (own0, own1)), (False, (xr0, xr1))):
        rows = pl.ds(pl.multiple_of(jnp.where(chip == 0, 0, HB) if mine else jnp.where(chip == 0, HB, 0), HB), HB)
        for i, part in enumerate(parts):
            cols = pl.ds(pl.multiple_of(core * half + i * quart, quart), quart)
            out_ref[rows, cols] = (hid_ref[rows, cols].astype(F32) + part[...]).astype(BF16)
    for mine, parts in ((True, (sown0, sown1)), (False, (sxr0, sxr1))):
        rows = pl.ds(pl.multiple_of(jnp.where(chip == 0, 0, HB) if mine else jnp.where(chip == 0, HB, 0), HB), HB)
        for i, part in enumerate(parts):
            cols = pl.ds(pl.multiple_of((1 - core) * half + i * quart, quart), quart)
            out_ref[rows, cols] = (hid_ref[rows, cols].astype(F32) + part[...]).astype(BF16)


def cost(us):
    return pl.CostEstimate(flops=int(us * 500e6), bytes_accessed=int(us * 3.3e6), transcendentals=0)


def vspec(n):
    return [pl.BlockSpec(memory_space=VM)] * n


def solution(mesh):
    core_pairs = [(0, 1), (1, 0), (2, 3), (3, 2)]
    chip_pairs = [(0, 2), (2, 0), (1, 3), (3, 1)]
    tp_pairs = [(0, 1), (1, 0)]
    params = lambda mib: pltpu.CompilerParams(vmem_limit_bytes=mib * 2 ** 20)

    def local_step(hidden, norm_gain, w_query, w_key, w_value, w_out, k_cache, v_cache, positions):
        half_dim = HD // 2
        inv_freq = 1.0 / (ROPE_BASE ** (jnp.arange(half_dim, dtype=F32) * 2.0 / HD))
        ang = positions.astype(F32)[:, None] * inv_freq[None, :]
        cosv, sinv = jnp.cos(ang), jnp.sin(ang)
        cosf = jnp.concatenate([cosv, cosv], axis=1)
        sinf = jnp.concatenate([-sinv, sinv], axis=1)

        kvm, vvm, keep0, send0 = pl.pallas_call(
            attn_kernel,
            in_specs=[pl.BlockSpec(memory_space=pltpu.SMEM)] + vspec(4) + [pl.BlockSpec(memory_space=pltpu.HBM)] * 5,
            out_specs=vspec(4),
            out_shape=[VM((B * RB, HD), BF16), VM((B * RB, HD), BF16),
                       VM((2, STAT, HD), F32), VM((2, STAT, HD), F32)],
            scratch_shapes=[
                VM((NSLOT, WROWS, NW), BF16), VM((B, NW), F32), VM((NWC, B, WROWS), BF16),
                VM((B * QL, HD), F32), VM((B * 16, HD), F32), VM((B * 16, HD), F32),
                VM((QL, RB), jnp.int32), VM((QL, HD), F32),
                pltpu.SemaphoreType.DMA((NSLOT, 3)), pltpu.SemaphoreType.DMA((NCC,)), pltpu.SemaphoreType.DMA((NCC,)),
            ],
            compiler_params=params(24),
            cost_estimate=cost(20),
            name="attn",
        )(positions, hidden, norm_gain.reshape(1, D), cosf, sinf, w_query, w_key, w_value,
          k_cache.reshape(B * RB, HD), v_cache.reshape(B * RB, HD))

        def write(x):
            return pl.pallas_call(
                write_kernel, in_specs=vspec(1), out_specs=pl.BlockSpec(memory_space=pltpu.HBM),
                out_shape=jax.ShapeDtypeStruct((B * RB, HD), BF16),
                scratch_shapes=[pltpu.SemaphoreType.DMA((8,))],
                compiler_params=params(4), cost_estimate=cost(5), name="write",
            )(x).reshape(k_cache.shape)

        recv0 = lax.ppermute(send0, "sp", core_pairs)
        keep1, send1 = pl.pallas_call(
            merge_kernel, in_specs=vspec(2), out_specs=vspec(2),
            out_shape=[jax.ShapeDtypeStruct((STAT, HD), F32)] * 2,
            compiler_params=params(4), cost_estimate=cost(0.5), name="merge",
        )(keep0, recv0)
        recv1 = lax.ppermute(send1, "sp", chip_pairs)
        k_out = write(kvm)
        o_own = pl.pallas_call(
            finish_kernel, in_specs=vspec(2), out_specs=vspec(1)[0],
            out_shape=jax.ShapeDtypeStruct((HB * 8, HD), F32),
            compiler_params=params(4), cost_estimate=cost(0.5), name="finish",
        )(keep1, recv1)
        o_sib = lax.ppermute(o_own, "sp", core_pairs)
        y0, y1 = pl.pallas_call(
            out_kernel, in_specs=vspec(2) + [pl.BlockSpec(memory_space=pltpu.HBM)], out_specs=vspec(2),
            out_shape=[jax.ShapeDtypeStruct((HB, D // 4), F32)] * 2,
            scratch_shapes=[VM((OC, QW // OC, D // 2), BF16), VM((HB, QW), BF16), pltpu.SemaphoreType.DMA((OC,))],
            compiler_params=params(12), cost_estimate=cost(3), name="outproj",
        )(o_own, o_sib, pltpu.with_memory_space_constraint(w_out, pltpu.HBM))
        own = [y + lax.ppermute(y, "tp", tp_pairs) for y in (y0, y1)]
        v_out = write(vvm)
        xr = [lax.ppermute(y, "sp", chip_pairs) for y in own]
        sib = [lax.ppermute(y, "sp", core_pairs) for y in own + xr]
        out = pl.pallas_call(
            final_kernel, in_specs=vspec(9), out_specs=vspec(1)[0],
            out_shape=jax.ShapeDtypeStruct((B, D), BF16),
            compiler_params=params(6), cost_estimate=cost(0.5), name="final",
        )(hidden, *own, *xr, *sib)
        return out, k_out, v_out

    cache_spec = P("dp", "sp", "tp", None)
    specs_in = (P("dp", None), P(None), P(None, "tp"), P(None, "tp"), P(None, "tp"), P("tp", None), cache_spec, cache_spec, P("dp"))
    specs_out = (P("dp", None), cache_spec, cache_spec)
    return jax.shard_map(local_step, mesh=mesh, in_specs=specs_in, out_specs=specs_out, check_vma=False)
```

time: 178 us -> 72.9 us (0.41)
  waiting for transfers between devices: 68.9 us -> 11 us
  Pallas kernels: 0 us -> 49.1 us
  matrix products: 43.9 us -> 0 us
  other arithmetic: 42.8 us -> 1.63 us
  between operations: 14.2 us -> 0.75 us
  starting transfers between devices: 0.08 us -> 10.4 us
  local copies, waits for them, and re-layouts: 7.57 us -> 0.01 us
    pallas_call x0 -> x7, Pallas kernels: none -> 49.1 us  [the longest x1 32 us: local_step(): pl.pallas_call(attn_kernel, in_specs=[pl.BlockSpec(memory_space=pltpu.SME...]
    dot_general x6 -> x0, matrix products: 43.9 us -> none  [the longest x1 10.4 us: local_step(): jnp.einsum('bkgd,bskd->bkgs', q_rot, k_updated, preferred_element_type=jn...]
    all_gather x1 -> x0, waiting for transfers between devices: 34.4 us -> none  [local_step(): gathered = lax.all_gather(block_stats, 'sp')]
    psum x1 -> x0, waiting for transfers between devices: 34.4 us -> none  [local_step(): proj_out = lax.psum(part_proj, 'tp')]
    select_n x1 -> x0, other arithmetic: 26.1 us -> none  [local_step(): v_updated = jnp.where(slot_mask, v_new[:, None], v_cache)]
    ppermute x0 -> x11, waiting for transfers between devices: none -> 11 us  [the longest x2 4.58 us: local_step(): own = [y + lax.ppermute(y, 'tp', tp_pairs) for y in (y0, y1)]]
    ppermute x0 -> x11, starting transfers between devices: none -> 10.4 us  [the longest x2 3.49 us: local_step(): xr = [lax.ppermute(y, 'sp', chip_pairs) for y in own]]
    slice x1 -> x0, other arithmetic: 5.41 us -> none  [local_step(): total_sum = jnp.sum(gathered[..., head_dim:head_dim + 1] * rescale, axis=0)]
  transfers between devices with their start and end apart: 2 -> 11, of which waited for: 2 -> 5; matrix products, arithmetic and copies ran while one was open for 0% -> 0% of each run, Pallas kernels for 0% -> 16%
where the time goes in v1:
time: 72.9 us; the launch traced here: 72.8 us
  Pallas kernels  49.1 us (67%)
  waiting for transfers between devices  11 us (15%)
  starting transfers between devices  10.4 us (14%)
  other arithmetic  1.63 us (2%)
  between operations  0.75 us (1%)
    pallas_call x1, Pallas kernels, local_step(): pl.pallas_call(attn_kernel, in_specs=[pl.BlockSpec(memory_space=pltpu.SME...  32 us
    pallas_call x2, Pallas kernels, write(): pl.pallas_call(write_kernel, in_specs=vspec(1), out_specs=pl.BlockSpec(me...  11.8 us
    ppermute x2, waiting for transfers between devices, local_step(): own = [y + lax.ppermute(y, 'tp', tp_pairs) for y in (y0, y1)]  4.58 us
    ppermute x1, waiting for transfers between devices, local_step(): recv1 = lax.ppermute(send1, 'sp', chip_pairs)  3.89 us
    pallas_call x1, Pallas kernels, local_step(): pl.pallas_call(out_kernel, in_specs=vspec(2) + [pl.BlockSpec(memory_space...  3.78 us
    ppermute x2, starting transfers between devices, local_step(): xr = [lax.ppermute(y, 'sp', chip_pairs) for y in own]  3.49 us
    ppermute x1, starting transfers between devices, local_step(): recv1 = lax.ppermute(send1, 'sp', chip_pairs)  2.88 us
    ppermute x2, starting transfers between devices, local_step(): own = [y + lax.ppermute(y, 'tp', tp_pairs) for y in (y0, y1)]  2.05 us
  transfers between devices with their start and end apart: 11, of which 5 were waited for; matrix products, arithmetic and copies ran while one was open for 0% of the time, Pallas kernels for 16%

profile of v1, /device:TPU:0, one launch (start us, length us, event | category | flops | bytes accessed | tf_op | source)
XLA Modules:
  0.0 72.8 jit_solution(834194619431579273)
XLA Ops:
  0.6 0.7 convert_element_type.3
  1.3 0.2 fusion
  1.5 0.7 pad_maximum_fusion
  2.2 32.0 %attn.1 = (bf16[65536,128]{1,0:T(8,128)(2,1)S(1)}, bf16[65536,128]{1,0:T(8,128)(2,1)S(1)}, f32[2,264,128]{2,1,0:T(8,128)S(1)}, f32[2,264,128]{2,1,0:T(8,128)S(1)}) custom-call(s32[64]{0:T(128)} %pos_ref.1, bf16[64,4096]{1,0:T(8,128)(2,1)} %hid_ref.3, f32[1,4096]{1,0:T(1,128)} %bitcast.9, f32[64,128]{1,0:T(8,128)} %get-tuple-element.22.cos_ref, ...), custom_call_target="tpu_custom_call" | custom-call | flops 10000000000 | bytes 66000000 | tf_op jit(solution)/shard_map/attn/pallas_call | solution.py:274
  34.2 0.9 %collective-permute-start = (f32[2,264,128]{2,1,0:T(8,128)S(1)}, f32[2,264,128]{2,1,0:T(8,128)S(1)}, u32[]{:S(2)}, u32[]{:S(2)}) collective-permute-start(f32[2,264,128]{2,1,0:T(8,128)S(1)} %get-tuple-element.12), channel_id=1, source_target_pairs={{0,1},{1,0},{2,3},{3,2},{4,5},{5,4},{6,7},{7,6}} | collective-permute-start | bytes 811016 | tf_op jit(solution)/shard_map/ppermute | solution.py:300
  35.1 1.2 %collective-permute-done.recv_in = f32[2,264,128]{2,1,0:T(8,128)S(1)} collective-permute-done((f32[2,264,128]{2,1,0:T(8,128)S(1)}, f32[2,264,128]{2,1,0:T(8,128)S(1)}, u32[]{:S(2)}, u32[]{:S(2)}) %collective-permute-start) | collective-permute-done | bytes 270368 | tf_op jit(solution)/shard_map/ppermute | solution.py:300
  36.2 0.3 merge.1
  36.5 2.9 %collective-permute-start.1 = (f32[264,128]{1,0:T(8,128)S(1)}, f32[264,128]{1,0:T(8,128)S(1)}, u32[]{:S(2)}, u32[]{:S(2)}) collective-permute-start(f32[264,128]{1,0:T(8,128)S(1)} %get-tuple-element.14), channel_id=1, source_target_pairs={{0,2},{2,0},{1,3},{3,1},{4,6},{6,4},{5,7},{7,5}} | collective-permute-start | bytes 405512 | tf_op jit(solution)/shard_map/ppermute | solution.py:306
  39.4 3.9 %collective-permute-done.1.recv_in = f32[264,128]{1,0:T(8,128)S(1)} collective-permute-done((f32[264,128]{1,0:T(8,128)S(1)}, f32[264,128]{1,0:T(8,128)S(1)}, u32[]{:S(2)}, u32[]{:S(2)}) %collective-permute-start.1) | collective-permute-done | bytes 135200 | tf_op jit(solution)/shard_map/ppermute | solution.py:306
  43.3 0.3 finish.1.own_ref
  43.6 0.0 collective-permute-start.2
  43.7 1.3 %collective-permute-done.2.sib_ref = f32[256,128]{1,0:T(8,128)S(1)} collective-permute-done((f32[256,128]{1,0:T(8,128)S(1)}, f32[256,128]{1,0:T(8,128)S(1)}, u32[]{:S(2)}, u32[]{:S(2)}) %collective-permute-start.2) | collective-permute-done | bytes 131104 | tf_op jit(solution)/shard_map/ppermute | solution.py:313
  45.0 3.8 %outproj.1 = (f32[32,1024]{1,0:T(8,128)S(1)}, f32[32,1024]{1,0:T(8,128)S(1)}) custom-call(f32[256,128]{1,0:T(8,128)S(1)} %finish.1.own_ref, f32[256,128]{1,0:T(8,128)S(1)} %collective-permute-done.2.sib_ref, bf16[2048,4096]{1,0:T(8,128)(2,1)} %wo.1), custom_call_target="tpu_custom_call" | custom-call | flops 1500000000 | bytes 9900000 | tf_op jit(solution)/shard_map/outproj/pallas_call | solution.py:314
  48.8 1.8 %collective-permute-start.3 = (f32[32,1024]{1,0:T(8,128)S(1)}, f32[32,1024]{1,0:T(8,128)S(1)}, u32[]{:S(2)}, u32[]{:S(2)}) collective-permute-start(f32[32,1024]{1,0:T(8,128)S(1)} %get-tuple-element.15), channel_id=1, source_target_pairs={{0,4},{4,0},{1,5},{5,1},{2,6},{6,2},{3,7},{7,3}} | collective-permute-start | bytes 393224 | tf_op jit(solution)/shard_map/ppermute | solution.py:320
  50.6 0.3 collective-permute-start.4
  50.8 4.3 %collective-permute-done.3 = f32[32,1024]{1,0:T(8,128)S(1)} collective-permute-done((f32[32,1024]{1,0:T(8,128)S(1)}, f32[32,1024]{1,0:T(8,128)S(1)}, u32[]{:S(2)}, u32[]{:S(2)}) %collective-permute-start.3) | collective-permute-done | bytes 131104 | tf_op jit(solution)/shard_map/ppermute | solution.py:320
  55.2 1.8 %collective-permute-start.5 = (f32[32,1024]{1,0:T(8,128)S(1)}, f32[32,1024]{1,0:T(8,128)S(1)}, u32[]{:S(2)}, u32[]{:S(2)}) collective-permute-start(f32[32,1024]{1,0:T(8,128)S(1)} %add.6.own0), channel_id=1, source_target_pairs={{0,2},{2,0},{1,3},{3,1},{4,6},{6,4},{5,7},{7,5}} | collective-permute-start | bytes 393224 | tf_op jit(solution)/shard_map/ppermute | solution.py:322
  57.0 0.2 collective-permute-done.4
  57.2 1.7 %collective-permute-start.6 = (f32[32,1024]{1,0:T(8,128)S(1)}, f32[32,1024]{1,0:T(8,128)S(1)}, u32[]{:S(2)}, u32[]{:S(2)}) collective-permute-start(f32[32,1024]{1,0:T(8,128)S(1)} %add.7.own1), channel_id=1, source_target_pairs={{0,2},{2,0},{1,3},{3,1},{4,6},{6,4},{5,7},{7,5}} | collective-permute-start | bytes 393224 | tf_op jit(solution)/shard_map/ppermute | solution.py:322
  58.9 5.9 %write.2 = bf16[65536,128]{1,0:T(8,128)(2,1)} custom-call(bf16[65536,128]{1,0:T(8,128)(2,1)S(1)} %get-tuple-element.17.src), custom_call_target="tpu_custom_call" | custom-call | flops 2500000000 | bytes 16500000 | tf_op jit(solution)/shard_map/write/pallas_call | solution.py:293
  64.9 0.0 collective-permute-start.7
  64.9 0.5 collective-permute-start.8
  65.4 0.0 collective-permute-done.5.xr0
  65.4 0.0 collective-permute-start.9
  65.4 0.0 collective-permute-done.6.xr1
  65.4 0.5 collective-permute-start.10
  65.9 5.9 %write.3 = bf16[65536,128]{1,0:T(8,128)(2,1)} custom-call(bf16[65536,128]{1,0:T(8,128)(2,1)S(1)} %get-tuple-element.18.src), custom_call_target="tpu_custom_call" | custom-call | flops 2500000000 | bytes 16500000 | tf_op jit(solution)/shard_map/write/pallas_call | solution.py:293
  71.8 0.0 collective-permute-done.7.sown0
  71.9 0.0 collective-permute-done.8.sown1
  71.9 0.0 collective-permute-done.9.sxr0
  71.9 0.0 collective-permute-done.10.sxr1
  71.9 0.9 %final.1 = bf16[64,4096]{1,0:T(8,128)(2,1)} custom-call(bf16[64,4096]{1,0:T(8,128)(2,1)S(1)} %copy-done, f32[32,1024]{1,0:T(8,128)S(1)} %add.6.own0, f32[32,1024]{1,0:T(8,128)S(1)} %add.7.own1, f32[32,1024]{1,0:T(8,128)S(1)} %collective-permute-done.5.xr0, f32[32,1024]{1,0:T(8,128)S(1)} %collective-permute-done.6.xr1, ...), custom_call_target="tpu_custom_call" | custom-call | flops 250000000 | bytes 1650000 | tf_op jit(solution)/shard_map/final/pallas_call | solution.py:324
  (5 shorter events, 0.1 us)
Async XLA Ops:
  34.2 2.1 %collective-permute-start = (f32[2,264,128]{2,1,0:T(8,128)S(1)}, f32[2,264,128]{2,1,0:T(8,128)S(1)}, u32[]{:S(2)}, u32[]{:S(2)}) collective-permute-start(f32[2,264,128]{2,1,0:T(8,128)S(1)} %get-tuple-element.12), channel_id=1, source_target_pairs={{0,1},{1,0},{2,3},{3,2},{4,5},{5,4},{6,7},{7,6}} | collective-permute-start | bytes 811016 | tf_op jit(solution)/shard_map/ppermute | solution.py:300
  36.5 6.8 %collective-permute-start.1 = (f32[264,128]{1,0:T(8,128)S(1)}, f32[264,128]{1,0:T(8,128)S(1)}, u32[]{:S(2)}, u32[]{:S(2)}) collective-permute-start(f32[264,128]{1,0:T(8,128)S(1)} %get-tuple-element.14), channel_id=1, source_target_pairs={{0,2},{2,0},{1,3},{3,1},{4,6},{6,4},{5,7},{7,5}} | collective-permute-start | bytes 405512 | tf_op jit(solution)/shard_map/ppermute | solution.py:306
  43.6 1.4 %collective-permute-start.2 = (f32[256,128]{1,0:T(8,128)S(1)}, f32[256,128]{1,0:T(8,128)S(1)}, u32[]{:S(2)}, u32[]{:S(2)}) collective-permute-start(f32[256,128]{1,0:T(8,128)S(1)} %finish.1.own_ref), channel_id=1, source_target_pairs={{0,1},{1,0},{2,3},{3,2},{4,5},{5,4},{6,7},{7,6}} | collective-permute-start | bytes 393224 | tf_op jit(solution)/shard_map/ppermute | solution.py:313
  48.8 6.4 %collective-permute-start.3 = (f32[32,1024]{1,0:T(8,128)S(1)}, f32[32,1024]{1,0:T(8,128)S(1)}, u32[]{:S(2)}, u32[]{:S(2)}) collective-permute-start(f32[32,1024]{1,0:T(8,128)S(1)} %get-tuple-element.15), channel_id=1, source_target_pairs={{0,4},{4,0},{1,5},{5,1},{2,6},{6,2},{3,7},{7,3}} | collective-permute-start | bytes 393224 | tf_op jit(solution)/shard_map/ppermute | solution.py:320
  50.6 6.6 %collective-permute-start.4 = (f32[32,1024]{1,0:T(8,128)S(1)}, f32[32,1024]{1,0:T(8,128)S(1)}, u32[]{:S(2)}, u32[]{:S(2)}) collective-permute-start(f32[32,1024]{1,0:T(8,128)S(1)} %get-tuple-element.16), channel_id=1, source_target_pairs={{0,4},{4,0},{1,5},{5,1},{2,6},{6,2},{3,7},{7,3}} | collective-permute-start | bytes 393224 | tf_op jit(solution)/shard_map/ppermute | solution.py:320
  55.2 10.2 %collective-permute-start.5 = (f32[32,1024]{1,0:T(8,128)S(1)}, f32[32,1024]{1,0:T(8,128)S(1)}, u32[]{:S(2)}, u32[]{:S(2)}) collective-permute-start(f32[32,1024]{1,0:T(8,128)S(1)} %add.6.own0), channel_id=1, source_target_pairs={{0,2},{2,0},{1,3},{3,1},{4,6},{6,4},{5,7},{7,5}} | collective-permute-start | bytes 393224 | tf_op jit(solution)/shard_map/ppermute | solution.py:322
  57.2 8.2 %collective-permute-start.6 = (f32[32,1024]{1,0:T(8,128)S(1)}, f32[32,1024]{1,0:T(8,128)S(1)}, u32[]{:S(2)}, u32[]{:S(2)}) collective-permute-start(f32[32,1024]{1,0:T(8,128)S(1)} %add.7.own1), channel_id=1, source_target_pairs={{0,2},{2,0},{1,3},{3,1},{4,6},{6,4},{5,7},{7,5}} | collective-permute-start | bytes 393224 | tf_op jit(solution)/shard_map/ppermute | solution.py:322
  64.9 7.0 %collective-permute-start.7 = (f32[32,1024]{1,0:T(8,128)S(1)}, f32[32,1024]{1,0:T(8,128)S(1)}, u32[]{:S(2)}, u32[]{:S(2)}) collective-permute-start(f32[32,1024]{1,0:T(8,128)S(1)} %add.6.own0), channel_id=1, source_target_pairs={{0,1},{1,0},{2,3},{3,2},{4,5},{5,4},{6,7},{7,6}} | collective-permute-start | bytes 393224 | tf_op jit(solution)/shard_map/ppermute | solution.py:323
  64.9 7.0 %collective-permute-start.8 = (f32[32,1024]{1,0:T(8,128)S(1)}, f32[32,1024]{1,0:T(8,128)S(1)}, u32[]{:S(2)}, u32[]{:S(2)}) collective-permute-start(f32[32,1024]{1,0:T(8,128)S(1)} %add.7.own1), channel_id=1, source_target_pairs={{0,1},{1,0},{2,3},{3,2},{4,5},{5,4},{6,7},{7,6}} | collective-permute-start | bytes 393224 | tf_op jit(solution)/shard_map/ppermute | solution.py:323
  65.4 6.5 %collective-permute-start.9 = (f32[32,1024]{1,0:T(8,128)S(1)}, f32[32,1024]{1,0:T(8,128)S(1)}, u32[]{:S(2)}, u32[]{:S(2)}) collective-permute-start(f32[32,1024]{1,0:T(8,128)S(1)} %collective-permute-done.5.xr0), channel_id=1, source_target_pairs={{0,1},{1,0},{2,3},{3,2},{4,5},{5,4},{6,7},{7,6}} | collective-permute-start | bytes 393224 | tf_op jit(solution)/shard_map/ppermute | solution.py:323
  65.4 6.4 %collective-permute-start.10 = (f32[32,1024]{1,0:T(8,128)S(1)}, f32[32,1024]{1,0:T(8,128)S(1)}, u32[]{:S(2)}, u32[]{:S(2)}) collective-permute-start(f32[32,1024]{1,0:T(8,128)S(1)} %collective-permute-done.6.xr1), channel_id=1, source_target_pairs={{0,1},{1,0},{2,3},{3,2},{4,5},{5,4},{6,7},{7,6}} | collective-permute-start | bytes 393224 | tf_op jit(solution)/shard_map/ppermute | solution.py:323
  65.9 6.0 %copy-start = (bf16[64,4096]{1,0:T(8,128)(2,1)S(1)}, bf16[64,4096]{1,0:T(8,128)(2,1)}, u32[]{:S(2)}) copy-start(bf16[64,4096]{1,0:T(8,128)(2,1)} %hid_ref.3) | copy-start | bytes 1572868
